TPU v7x, 32 devices: a whole 2x2x4 slice. The times are simulated.
32 devices in a mesh: kpt: 2 (over y), row: 8 (over z, x), freq: 2 (over core).
Axes of the slice: x: 2, y: 2, z: 4, core: 2. Of those that a mesh axis runs over, the one named last changes fastest.
Arguments:
- screened: bfloat16 [8, 2, 8192, 8192], P(('kpt', 'freq'), None, 'row'), parts along dimension 0, may hold values from -0.0625 to 0.0625
- elements: bfloat16 [2, 1024, 8192], P(None, 'kpt', 'row'), parts along dimension 1, may hold values from -0.59765625 to 0.59765625
- node_freq: float32 [4], P('freq'), may hold values from 0.1 to 2
- node_weight: float32 [4], P('freq'), may hold values from 0.1 to 1
- band_energy: float32 [1024], P('kpt'), parts along dimension 0, may hold values from -1 to 1
- energy_grid: float32 [64], replicated, may hold values from -1 to 1
- pair_state: int32 [1024], P('kpt'), parts along dimension 0, may hold values from 0 to 31
- pair_band: int32 [1024], P('kpt'), parts along dimension 0, may hold values from 0 to 511
Outputs:
- sigma: float32 [2, 64, 64], P(None, 'kpt'), parts along dimension 1
There are 2 independent parts, one for each index of `kpt`. A program takes and returns all parts, laid end to end along the dimension named above; an argument that names none is the same for every part. Nothing has to cross between parts.
All inputs are finite; a program needn't handle non-finite values.
Results may differ from a plain program's by a relative error of at most 0.0003.
Values may be sent and summed in bfloat16 or wider, within the bound.
A program may use at most 192 MiB of HBM per device.

v0:
```python
import functools

import jax
import jax.numpy as jnp
from jax import lax
from jax.experimental import pallas as pl
from jax.experimental.pallas import tpu as pltpu
from jax.sharding import PartitionSpec as P

NSTATE = 32
TILE = 512
DEPTH = 4


def product(weights, piece):
    return jnp.einsum("jgc,pc->jgp", weights, piece, preferred_element_type=jnp.float32)


def self_energy(
    form_re, form_im, node_freq, node_weight, band_energy, energy_grid, pair_state, pair_band
):
    band_onehot = (
        pair_band[:, None] == jnp.arange(band_energy.shape[0], dtype=jnp.int32)[None, :]
    ).astype(jnp.float32)
    pair_eps = jnp.dot(band_onehot, band_energy, precision=lax.Precision.HIGHEST)
    delta = energy_grid[None, :] - pair_eps[:, None]
    factor = (
        node_weight[:, None, None]
        * delta[None]
        / (delta[None] ** 2 + node_freq[:, None, None] ** 2)
    )
    terms_re = jnp.sum(form_re[:, :, None] * factor, axis=0)
    terms_im = jnp.sum(form_im[:, :, None] * factor, axis=0)
    state_onehot = (jnp.arange(NSTATE, dtype=jnp.int32)[:, None] == pair_state[None, :]).astype(
        jnp.float32
    )
    sig_re = jnp.dot(state_onehot, terms_re, precision=lax.Precision.HIGHEST)
    sig_im = jnp.dot(state_onehot, terms_im, precision=lax.Precision.HIGHEST)
    return jnp.stack([sig_re, sig_im])


def ring_position(idx, n):
    par = idx % 2
    return (1 - par) * (idx // 2) + par * (n - 1 - idx // 2)


def ring_index(pos, n):
    high = pos // (n // 2)
    return (1 - high) * (2 * pos) + high * (2 * (n - 1 - pos) + 1)


def ring_kernel(
    n, nodes, rows, chunk, wide, tile, depth,
    w_hbm, m_hbm, param_ref, out_ref,
    block, held, wbuf, rhs, acc, forms, peers, twin,
    own_sem, w_sem, send_sem, recv_sem, sib_send, sib_recv,
    form_send, form_recv, twin_send, twin_recv,
):
    me = lax.axis_index("row")
    core = lax.axis_index("freq")
    pos = ring_position(me, n)
    right = ring_index((pos + 1) % n, n)
    left = ring_index((pos + n - 1) % n, n)
    other = 1 - core
    half = wide // 2
    units = 2 * n

    def item(step, way):
        hop = (step + 1) // 2
        first = (step + 1) % 2
        owner_pos = (pos + n + (2 * way - 1) * hop) % n
        part = (1 - way) * first + way * (1 - first)
        return ring_index(owner_pos, n), part

    def w_copies(unit):
        owner, part = item(unit // 2, unit % 2)
        slot = unit % depth
        start = pl.multiple_of(owner * 2 * chunk + part * chunk, 128)
        return [
            pltpu.make_async_copy(
                w_hbm.at[j, c, :, pl.ds(start, chunk)],
                wbuf.at[slot, j, :, pl.ds(c * chunk, chunk)],
                w_sem.at[slot, j, c],
            )
            for j in range(nodes)
            for c in range(2)
        ]

    def send(step, way, owner, part):
        ref = held.at[owner, part, core]
        return pltpu.make_async_remote_copy(
            src_ref=ref,
            dst_ref=ref,
            send_sem=send_sem.at[step, way],
            recv_sem=recv_sem.at[step, way],
            device_id={"row": right if way == 0 else left},
            device_id_type=pl.DeviceIdType.MESH,
        )

    def pass_over(step, way, owner, part, core_of):
        ref = held.at[owner, part, core_of]
        return pltpu.make_async_remote_copy(
            src_ref=ref,
            dst_ref=ref,
            send_sem=sib_send.at[step, way],
            recv_sem=sib_recv.at[step, way],
            device_id={"freq": other},
            device_id_type=pl.DeviceIdType.MESH,
        )

    own = pltpu.make_async_copy(m_hbm, block, own_sem)
    own.start()
    for unit in range(depth - 1):
        for copy in w_copies(unit):
            copy.start()
    barrier = pltpu.get_barrier_semaphore()
    for hop in range(1, n):
        pl.semaphore_signal(
            barrier, device_id={"row": (me + hop) % n}, device_id_type=pl.DeviceIdType.MESH
        )
    pl.semaphore_signal(barrier, device_id={"freq": other}, device_id_type=pl.DeviceIdType.MESH)
    own.wait()

    def turn(part, f):
        pairs = pl.ds(pl.multiple_of(f * half, half), half)
        for c in range(2):
            piece = block[c, pairs, part * chunk : (part + 1) * chunk]
            held[me, part, f, :, c * half : (c + 1) * half] = piece.T

    turn(0, core)
    turn(1, core)
    pl.semaphore_wait(barrier, n)
    for step in (1, 2):
        for way in (0, 1):
            part = (step + 1) % 2 if way == 0 else 1 - (step + 1) % 2
            send(step, way, me, part).start()
    turn(0, other)
    turn(1, other)
    acc[...] = jnp.zeros_like(acc)

    def compute(unit):
        slot = unit % depth
        owner, part = item(unit // 2, unit % 2)
        for f in range(2):
            rhs[f, :chunk, :] = held[owner, part, f]
            rhs[f, chunk:, :half] = -held[owner, part, f, :, half:]
            rhs[f, chunk:, half:] = held[owner, part, f, :, :half]
        for copy in w_copies(unit):
            copy.wait()

        @pl.when(unit + depth - 1 < units)
        def _():
            for copy in w_copies(unit + depth - 1):
                copy.start()

        tiles = rows // tile

        def one(i, carry):
            j = i // (2 * tiles)
            f = (i // tiles) % 2
            t = i % tiles
            spot = pl.ds(pl.multiple_of(t * tile, tile), tile)
            y = jnp.dot(wbuf[slot, j, spot, :], rhs[f], preferred_element_type=jnp.float32)
            per = chunk // tile
            mine = pl.ds(pl.multiple_of((t % per) * tile, tile), tile)
            m = held[me, t // per, f, mine, :].astype(jnp.float32)
            r, s = m[:, :half], m[:, half:]
            yr, yi = y[:, :half], y[:, half:]
            acc[0, j, f] += jnp.sum((r * yr + s * yi).reshape(tile // 8, 8, half), axis=0)
            acc[1, j, f] += jnp.sum((r * yi - s * yr).reshape(tile // 8, 8, half), axis=0)
            return carry

        lax.fori_loop(0, nodes * 2 * tiles, one, 0, unroll=4)

    def step_body(step, carry):
        @pl.when(step >= 1)
        def _():
            for way in (0, 1):
                owner, part = item(step, way)
                send(step, way, owner, part).wait_recv()

                @pl.when(step + 2 < n)
                def _():
                    send(step + 2, way, owner, part).start()

                pass_over(step, way, owner, part, core).start()
            for way in (0, 1):
                owner, part = item(step, way)
                pass_over(step, way, owner, part, other).wait_recv()

        def each(way, c):
            compute(2 * step + way)
            return c

        lax.fori_loop(0, 2, each, 0)
        return carry

    lax.fori_loop(0, n, step_body, 0)

    lines = 2 * nodes * 2
    forms[:lines, :] = jnp.sum(acc[...], axis=3).reshape(lines, half)
    forms[lines:, :] = jnp.zeros_like(forms[lines:, :])

    def spread(hop):
        return pltpu.make_async_remote_copy(
            src_ref=forms,
            dst_ref=peers.at[hop - 1],
            send_sem=form_send.at[hop - 1],
            recv_sem=form_recv.at[hop - 1],
            device_id={"row": (me + hop) % n},
            device_id_type=pl.DeviceIdType.MESH,
        )

    for hop in range(1, n):
        spread(hop).start()
    def drain(step, carry):
        for way in (0, 1):
            owner, part = item(step, way)
            send(step, way, owner, part).wait_send()
            pass_over(step, way, owner, part, core).wait_send()
        return carry

    lax.fori_loop(1, n, drain, 0)
    total = forms[...]
    for hop in range(1, n):
        spread(hop).wait()
        total += peers[hop - 1]
    twin[0, :lines, :] = total[:lines, :]
    twin[0, lines:, :] = param_ref[...]
    swap = pltpu.make_async_remote_copy(
        src_ref=twin.at[0],
        dst_ref=twin.at[1],
        send_sem=twin_send,
        recv_sem=twin_recv,
        device_id={"freq": other},
        device_id_type=pl.DeviceIdType.MESH,
    )
    swap.start()
    out_ref[0] = twin[0]
    swap.wait()
    out_ref[1] = twin[1]


def ring_forms(screened, elements, node_freq, node_weight):
    nodes, _, rows, ng = screened.shape
    n = lax.axis_size("row")
    npair = elements.shape[1]
    block = elements.shape[2]
    chunk = block // 2
    half = npair // 2
    tile = min(TILE, chunk)
    depth = DEPTH
    lines = 2 * nodes * 2
    spare = -(-2 * nodes // 8) * 8
    params = jnp.concatenate([node_freq, node_weight])
    params = jnp.pad(params, (0, spare - 2 * nodes))
    params = jnp.broadcast_to(params[:, None], (spare, half))
    out = pl.pallas_call(
        functools.partial(ring_kernel, n, nodes, rows, chunk, npair, tile, depth),
        out_shape=jax.ShapeDtypeStruct((2, lines + spare, half), jnp.float32),
        in_specs=[
            pl.BlockSpec(memory_space=pl.ANY),
            pl.BlockSpec(memory_space=pl.ANY),
            pl.BlockSpec(memory_space=pltpu.VMEM),
        ],
        out_specs=pl.BlockSpec(memory_space=pltpu.VMEM),
        scratch_shapes=[
            pltpu.VMEM((2, npair, block), jnp.bfloat16),
            pltpu.VMEM((n, 2, 2, chunk, npair), jnp.bfloat16),
            pltpu.VMEM((depth, nodes, rows, 2 * chunk), jnp.bfloat16),
            pltpu.VMEM((2, 2 * chunk, npair), jnp.bfloat16),
            pltpu.VMEM((2, nodes, 2, 8, half), jnp.float32),
            pltpu.VMEM((lines + spare, half), jnp.float32),
            pltpu.VMEM((n - 1, lines + spare, half), jnp.float32),
            pltpu.VMEM((2, lines + spare, half), jnp.float32),
            pltpu.SemaphoreType.DMA,
            pltpu.SemaphoreType.DMA((depth, nodes, 2)),
            pltpu.SemaphoreType.DMA((n, 2)),
            pltpu.SemaphoreType.DMA((n, 2)),
            pltpu.SemaphoreType.DMA((n, 2)),
            pltpu.SemaphoreType.DMA((n, 2)),
            pltpu.SemaphoreType.DMA((n - 1,)),
            pltpu.SemaphoreType.DMA((n - 1,)),
            pltpu.SemaphoreType.DMA,
            pltpu.SemaphoreType.DMA,
        ],
        compiler_params=pltpu.CompilerParams(
            collective_id=0, has_side_effects=True, vmem_limit_bytes=62 * 1024 * 1024
        ),
    )(screened, elements, params)
    forms = out[:, :lines].reshape(2, 2, nodes, npair).transpose(1, 0, 2, 3)
    forms = forms.reshape(2, 2 * nodes, npair)
    freqs = out[:, lines : lines + nodes, 0].reshape(-1)
    weights = out[:, lines + nodes : lines + 2 * nodes, 0].reshape(-1)
    return forms[0], forms[1], freqs, weights


def per_device(
    screened, elements, node_freq, node_weight, band_energy, energy_grid, pair_state, pair_band
):
    n = lax.axis_size("row")
    two = n >= 4 and n % 2 == 0 and lax.axis_size("freq") == 2
    if two and elements.shape[2] % 256 == 0 and elements.shape[1] % 256 == 0:
        form_re, form_im, freqs, weights = ring_forms(screened, elements, node_freq, node_weight)
        return self_energy(
            form_re, form_im, freqs, weights, band_energy, energy_grid, pair_state, pair_band
        )
    w_real = screened[:, 0]
    w_imag = screened[:, 1]
    npair = elements.shape[1]
    half = npair // lax.axis_size("freq")
    mine = lax.dynamic_slice_in_dim(elements, lax.axis_index("freq") * half, half, 1)
    collected = lax.all_gather(mine, "row", axis=2, tiled=True)
    piece = lax.all_gather(collected, "freq", axis=1, tiled=True)
    part_real = product(w_real, piece[0]) - product(w_imag, piece[1])
    part_imag = product(w_real, piece[1]) + product(w_imag, piece[0])
    stacked = jnp.stack([part_real, part_imag])
    y_real = stacked[0]
    y_imag = stacked[1]
    own_real = elements[0].T.astype(jnp.float32)[None]
    own_imag = elements[1].T.astype(jnp.float32)[None]
    form_re = jnp.sum(own_real * y_real + own_imag * y_imag, axis=1)
    form_im = jnp.sum(own_real * y_imag - own_imag * y_real, axis=1)
    form_re, form_im = lax.psum((form_re, form_im), "row")
    partial_sigma = self_energy(
        form_re, form_im, node_freq, node_weight, band_energy, energy_grid, pair_state, pair_band
    )
    return lax.psum(partial_sigma, "freq")


def solution(mesh):
    in_specs = (
        P(("kpt", "freq"), None, "row", None),
        P(None, "kpt", "row"),
        P("freq"),
        P("freq"),
        P("kpt"),
        P(),
        P("kpt"),
        P("kpt"),
    )
    out_specs = P(None, "kpt", None)
    return jax.shard_map(
        per_device, mesh=mesh, in_specs=in_specs, out_specs=out_specs, check_vma=False
    )
```

profile of v0, /device:TPU:0, one launch (start us, length us, event | category | flops | bytes accessed | tf_op | source)
XLA Modules:
  0.0 124.8 jit_solution(7275689429785151946)
XLA Ops:
  0.0 0.0 copy-start
  0.0 0.0 copy-start.1
  0.0 0.0 copy-start.2
  0.0 0.7 copy-done
  0.7 0.7 fusion.5
  1.4 1.3 %fusion = f32[1,512]{1,0:T(1,128)S(1)} fusion(f32[512,1]{0,1:T(1,128)S(1)} %bitcast.14, s32[512]{0:T(512)} %param.15), kind=kOutput, calls=%fused_computation.3 | convolution fusion | flops 3407872 | bytes 6144 | tf_op jit(solution)/shard_map/dot_general | solution.py:25
  2.7 0.7 broadcast_in_dim.2.param_ref
  3.4 118.2 %shard_map.82 = f32[2,16,256]{2,1,0:T(8,128)} custom-call(bf16[2,2,1024,8192]{3,2,1,0:T(8,128)(2,1)} %w_hbm.1, bf16[2,512,1024]{2,1,0:T(8,128)(2,1)} %m_hbm.1, f32[8,256]{1,0:T(8,128)} %broadcast_in_dim.2.param_ref), custom_call_target="tpu_custom_call" | custom-call | tf_op jit(solution)/shard_map/pallas_call | solution.py:258
  121.6 0.9 slice_reduce_fusion
  122.5 0.7 slice.17
  123.2 0.1 mul.37
  123.3 0.1 integer_pow.21
  123.4 0.0 copy-done.2
  123.4 0.1 broadcast_subtract_fusion
  123.5 0.2 multiply_reduce_fusion.1
  123.7 0.0 copy-done.1
  123.7 0.2 convolution_bitcast_fusion.1
  123.9 0.2 convolution_bitcast_fusion
  124.1 0.6 pad_maximum_fusion
  (4 shorter events, 0.1 us)
Async XLA Ops:
  0.0 0.7 copy-start
  0.0 123.7 %copy-start.1 = (s32[512]{0:T(512)S(1)}, s32[512]{0:T(512)}, u32[]{:S(2)}) copy-start(s32[512]{0:T(512)} %param.14) | copy-start | bytes 6148
  0.0 123.4 %copy-start.2 = (f32[64]{0:T(128)S(1)}, f32[64]{0:T(128)}, u32[]{:S(2)}) copy-start(f32[64]{0:T(128)} %param.13) | copy-start | bytes 772
where the time goes:
time: 125 us
  Pallas kernels  118 us (94%)
  other arithmetic  2.52 us (2%)
  local copies, waits for them, and re-layouts  2.3 us (2%)
  matrix products  1.7 us (1%)
    pallas_call x1, Pallas kernels, ring_forms(): pl.pallas_call(functools.partial(ring_kernel, n, nodes, rows, chunk, npai...  118 us

commit v1 on v0

v1 whole, which is shorter than its diff:
```python
import functools

import jax
import jax.numpy as jnp
from jax import lax
from jax.experimental import pallas as pl
from jax.experimental.pallas import tpu as pltpu
from jax.sharding import PartitionSpec as P

NSTATE = 32
LANES = 256
ROWS = 64
MESH = pl.DeviceIdType.MESH
NT = (((1,), (1,)), ((), ()))


def product(weights, piece):
    return jnp.einsum("jgc,pc->jgp", weights, piece, preferred_element_type=jnp.float32)


def self_energy(
    form_re, form_im, node_freq, node_weight, band_energy, energy_grid, pair_state, pair_band
):
    band_onehot = (
        pair_band[:, None] == jnp.arange(band_energy.shape[0], dtype=jnp.int32)[None, :]
    ).astype(jnp.float32)
    pair_eps = jnp.dot(band_onehot, band_energy, precision=lax.Precision.HIGHEST)
    delta = energy_grid[None, :] - pair_eps[:, None]
    factor = (
        node_weight[:, None, None]
        * delta[None]
        / (delta[None] ** 2 + node_freq[:, None, None] ** 2)
    )
    terms_re = jnp.sum(form_re[:, :, None] * factor, axis=0)
    terms_im = jnp.sum(form_im[:, :, None] * factor, axis=0)
    state_onehot = (jnp.arange(NSTATE, dtype=jnp.int32)[:, None] == pair_state[None, :]).astype(
        jnp.float32
    )
    sig_re = jnp.dot(state_onehot, terms_re, precision=lax.Precision.HIGHEST)
    sig_im = jnp.dot(state_onehot, terms_im, precision=lax.Precision.HIGHEST)
    return jnp.stack([sig_re, sig_im])


def ring_position(idx, n):
    par = idx % 2
    return (1 - par) * (idx // 2) + par * (n - 1 - idx // 2)


def ring_index(pos, n):
    high = pos // (n // 2)
    return (1 - high) * (2 * pos) + high * (2 * (n - 1 - pos) + 1)


def thirds(x):
    high = x.astype(jnp.bfloat16)
    rest = x - high.astype(jnp.float32)
    mid = rest.astype(jnp.bfloat16)
    low = (rest - mid.astype(jnp.float32)).astype(jnp.bfloat16)
    return high, mid, low


def forms_kernel(
    n, nodes, npair, block, lanes, lines,
    w_hbm, m_hbm, freq_hbm, weight_hbm, band_hbm, grid_hbm, state_hbm, pband_hbm,
    out_ref,
    lhs, held, wbuf, zbuf, acc, factor, onehot, forms, peers, twin,
    freq_v, weight_v, band_v, grid_v, state_v, pband_v,
    small_sem, lhs_sem, own_sem, other_sem, w_sem,
    send_sem, recv_sem, sib_send, sib_recv, form_send, form_recv, twin_send, twin_recv,
):
    me = lax.axis_index("row")
    core = lax.axis_index("freq")
    pos = ring_position(me, n)
    right = ring_index((pos + 1) % n, n)
    left = ring_index((pos + n - 1) % n, n)
    other = 1 - core
    half = npair // 2
    subs = block // lanes // 2
    rounds = n * subs

    def item(step, way, hop):
        first = (step + 1) % 2
        owner_pos = (pos + n + (2 * way - 1) * hop) % n
        part = (1 - way) * first + way * (1 - first)
        return ring_index(owner_pos, n), part

    def piece_of(rnd, way):
        step = rnd // subs
        owner, part = item(step, way, (step + 1) // 2)
        return owner, part * subs + rnd % subs

    def w_copies(rnd):
        copies = []
        for way in range(2):
            owner, q = piece_of(rnd, way)
            start = pl.multiple_of(owner * block + q * lanes, 128)
            for j in range(nodes):
                for c in range(2):
                    copies.append(
                        pltpu.make_async_copy(
                            w_hbm.at[j, c, :, pl.ds(start, lanes)],
                            wbuf.at[rnd % 2, way, pl.ds(c * block, block), pl.ds(j * lanes, lanes)],
                            w_sem.at[rnd % 2, way, j, c],
                        )
                    )
        return copies

    def send(rnd, way, owner, q):
        ref = held.at[owner, q, core]
        return pltpu.make_async_remote_copy(
            src_ref=ref,
            dst_ref=ref,
            send_sem=send_sem.at[rnd, way],
            recv_sem=recv_sem.at[rnd, way],
            device_id={"row": right if way == 0 else left},
            device_id_type=MESH,
        )

    def pass_over(rnd, way, owner, q, core_of):
        ref = held.at[owner, q, core_of]
        return pltpu.make_async_remote_copy(
            src_ref=ref,
            dst_ref=ref,
            send_sem=sib_send.at[rnd, way],
            recv_sem=sib_recv.at[rnd, way],
            device_id={"freq": other},
            device_id_type=MESH,
        )

    def own_copy(q, f, sem):
        return pltpu.make_async_copy(
            m_hbm.at[
                :,
                pl.ds(pl.multiple_of(f * half, half), half),
                pl.ds(q * lanes, lanes),
            ],
            held.at[me, q, f],
            sem.at[q],
        )

    barrier = pltpu.get_barrier_semaphore()
    for peer in (right, left):
        pl.semaphore_signal(barrier, device_id={"row": peer}, device_id_type=MESH)
    pl.semaphore_signal(barrier, device_id={"freq": other}, device_id_type=MESH)
    order = [p * subs + k for k in range(subs) for p in range(2)]
    for q in order:
        own_copy(q, core, own_sem).start()
    lhs_copies = [
        pltpu.make_async_copy(
            m_hbm.at[c], lhs.at[0, :, pl.ds(c * block, block)], lhs_sem.at[c]
        )
        for c in range(2)
    ]
    for copy in lhs_copies:
        copy.start()
    for copy in w_copies(0):
        copy.start()
    smalls = [
        pltpu.make_async_copy(src, dst, small_sem.at[i])
        for i, (src, dst) in enumerate(
            [
                (pband_hbm, pband_v), (band_hbm, band_v), (grid_hbm, grid_v),
                (state_hbm, state_v), (freq_hbm, freq_v), (weight_hbm, weight_v),
            ]
        )
    ]
    for copy in smalls:
        copy.start()
    for q in order:
        own_copy(q, other, other_sem).start()
    pl.semaphore_wait(barrier, 3)

    for q in order:
        own_copy(q, core, own_sem).wait()
        for step in (1, 2):
            for way in (0, 1):
                first = (step + 1) % 2
                part = first if way == 0 else 1 - first
                if q // subs == part:
                    send(step * subs + q % subs, way, me, q).start()

    for copy in smalls:
        copy.wait()
    nband = band_v.shape[1]
    band_of = lax.broadcasted_iota(jnp.int32, (nband, npair), 0)
    chosen = jnp.where(band_of == pband_v[...], 1.0, 0.0).astype(jnp.bfloat16)
    pair_eps = sum(
        jnp.dot(
            jnp.broadcast_to(part, (8, nband)), chosen, preferred_element_type=jnp.float32
        )
        for part in thirds(band_v[...])
    )[:1]
    ne = grid_v.shape[1]
    spot = lax.broadcasted_iota(jnp.int32, (ne, ne), 0) == lax.broadcasted_iota(
        jnp.int32, (ne, ne), 1
    )
    energy = jnp.sum(jnp.where(spot, jnp.broadcast_to(grid_v[...], (ne, ne)), 0.0), 1, keepdims=True)
    delta = energy - pair_eps
    for j in range(nodes):
        nu = freq_v[:, j : j + 1]
        factor[j] = weight_v[:, j : j + 1] * delta / (delta * delta + nu * nu)
    state_of = lax.broadcasted_iota(jnp.int32, (NSTATE, npair), 0)
    onehot[...] = jnp.where(state_of == state_v[...], 1.0, 0.0).astype(jnp.bfloat16)
    acc[...] = jnp.zeros_like(acc)

    for copy in lhs_copies:
        copy.wait()
    lhs[1, :, :block] = -lhs[0, :, block:]
    lhs[1, :, block:] = lhs[0, :, :block]
    for q in order:
        own_copy(q, other, other_sem).wait()

    def transfers(rnd):
        got = rnd - 1

        @pl.when((got >= subs) & (got < rounds))
        def _():
            for way in (0, 1):
                owner, q = piece_of(got, way)
                send(got, way, owner, q).wait_recv()

                @pl.when(got + 2 * subs < rounds)
                def _():
                    send(got + 2 * subs, way, owner, q).start()

                pass_over(got, way, owner, q, core).start()

        done = rnd - 2

        @pl.when(done >= subs)
        def _():
            for way in (0, 1):
                owner, q = piece_of(done, way)
                pass_over(done, way, owner, q, other).wait_recv()

    def weights(rnd):
        @pl.when(rnd + 1 < rounds)
        def _():
            for copy in w_copies(rnd + 1):
                copy.start()

        for copy in w_copies(rnd):
            copy.wait()

    def multiply(rnd):
        for way in (0, 1):
            for v in range(2):
                zbuf[rnd % 2, way, v] = jnp.dot(
                    lhs[v], wbuf[rnd % 2, way], preferred_element_type=jnp.float32
                )

    def combine(rnd):
        for way in (0, 1):
            owner, q = piece_of(rnd, way)
            for f in range(2):
                for t in range(half // ROWS):
                    spots = pl.ds(t * ROWS, ROWS)
                    pairs = pl.ds(f * half + t * ROWS, ROWS)
                    r = held[owner, q, f, 0, spots, :].astype(jnp.float32)
                    s = held[owner, q, f, 1, spots, :].astype(jnp.float32)
                    for j in range(nodes):
                        zr = zbuf[rnd % 2, way, 0, pairs, j * lanes : (j + 1) * lanes]
                        zi = zbuf[rnd % 2, way, 1, pairs, j * lanes : (j + 1) * lanes]
                        re = zr * r - zi * s
                        im = zr * s + zi * r
                        acc[0, j, pairs, :] += sum(
                            re[:, i * 128 : (i + 1) * 128] for i in range(lanes // 128)
                        )
                        acc[1, j, pairs, :] += sum(
                            im[:, i * 128 : (i + 1) * 128] for i in range(lanes // 128)
                        )

    def opening(rnd, carry):
        transfers(rnd)
        weights(rnd)
        multiply(rnd)
        return carry

    def middle(rnd, carry):
        transfers(rnd)
        weights(rnd)
        combine(rnd - 2)
        multiply(rnd)
        return carry

    def closing(rnd, carry):
        transfers(rnd)
        combine(rnd - 2)
        return carry

    lax.fori_loop(0, 2, opening, 0)
    lax.fori_loop(2, rounds, middle, 0)
    lax.fori_loop(rounds, rounds + 2, closing, 0)

    line_of = lax.broadcasted_iota(jnp.int32, (lines, 3 * 128), 0)
    total = jnp.zeros((lines, half), jnp.float32)
    for c in range(2):
        for j in range(nodes):
            for f in range(2):
                parts = jnp.concatenate(thirds(acc[c, j, f * half : (f + 1) * half, :]), axis=1)
                pick = jnp.where(line_of == (c * nodes + j) * 2 + f, 1.0, 0.0).astype(jnp.bfloat16)
                total += lax.dot_general(pick, parts, NT, preferred_element_type=jnp.float32)
    forms[...] = total

    def drain(rnd, carry):
        for way in (0, 1):
            owner, q = piece_of(rnd, way)
            send(rnd, way, owner, q).wait_send()
            pass_over(rnd, way, owner, q, core).wait_send()
        return carry

    lax.fori_loop(subs, rounds, drain, 0)

    def spread(hop):
        return pltpu.make_async_remote_copy(
            src_ref=forms,
            dst_ref=peers.at[hop - 1],
            send_sem=form_send.at[hop - 1],
            recv_sem=form_recv.at[hop - 1],
            device_id={"row": (me + hop) % n},
            device_id_type=MESH,
        )

    for hop in range(1, n):
        spread(hop).start()
    total = forms[...]
    for hop in range(1, n):
        spread(hop).wait()
        total += peers[hop - 1]
    for c in range(2):
        sigma = jnp.zeros((NSTATE, ne), jnp.float32)
        for f in range(2):
            pairs = slice(f * half, (f + 1) * half)
            terms = sum(
                total[(c * nodes + j) * 2 + f : (c * nodes + j) * 2 + f + 1, :]
                * factor[j, :, pairs]
                for j in range(nodes)
            )
            for part in thirds(terms):
                sigma += lax.dot_general(
                    onehot[:, pairs], part, NT, preferred_element_type=jnp.float32
                )
        twin[0, c] = sigma
    swap = pltpu.make_async_remote_copy(
        src_ref=twin.at[0],
        dst_ref=twin.at[1],
        send_sem=twin_send,
        recv_sem=twin_recv,
        device_id={"freq": other},
        device_id_type=MESH,
    )
    swap.start()
    swap.wait()
    out_ref[...] = twin[0] + twin[1]


def ring_sigma(
    screened, elements, node_freq, node_weight, band_energy, energy_grid, pair_state, pair_band
):
    nodes = screened.shape[0]
    n = lax.axis_size("row")
    npair = elements.shape[1]
    block = elements.shape[2]
    half = npair // 2
    ne = energy_grid.shape[0]
    nband = band_energy.shape[0]
    lines = -(-4 * nodes // 8) * 8
    pieces = block // LANES
    rounds = n * pieces // 2
    dma = pltpu.SemaphoreType.DMA
    return pl.pallas_call(
        functools.partial(forms_kernel, n, nodes, npair, block, LANES, lines),
        out_shape=jax.ShapeDtypeStruct((2, NSTATE, ne), jnp.float32),
        in_specs=[pl.BlockSpec(memory_space=pl.ANY)] * 8,
        out_specs=pl.BlockSpec(memory_space=pltpu.VMEM),
        scratch_shapes=[
            pltpu.VMEM((2, npair, 2 * block), jnp.bfloat16),
            pltpu.VMEM((n, pieces, 2, 2, half, LANES), jnp.bfloat16),
            pltpu.VMEM((2, 2, 2 * block, nodes * LANES), jnp.bfloat16),
            pltpu.VMEM((2, 2, 2, npair, nodes * LANES), jnp.float32),
            pltpu.VMEM((2, nodes, npair, 128), jnp.float32),
            pltpu.VMEM((nodes, ne, npair), jnp.float32),
            pltpu.VMEM((NSTATE, npair), jnp.bfloat16),
            pltpu.VMEM((lines, half), jnp.float32),
            pltpu.VMEM((n - 1, lines, half), jnp.float32),
            pltpu.VMEM((2, 2, NSTATE, ne), jnp.float32),
            pltpu.VMEM((1, nodes), jnp.float32),
            pltpu.VMEM((1, nodes), jnp.float32),
            pltpu.VMEM((1, nband), jnp.float32),
            pltpu.VMEM((1, ne), jnp.float32),
            pltpu.VMEM((1, npair), jnp.int32),
            pltpu.VMEM((1, npair), jnp.int32),
            dma((6,)),
            dma((2,)),
            dma((pieces,)),
            dma((pieces,)),
            dma((2, 2, nodes, 2)),
            dma((rounds, 2)),
            dma((rounds, 2)),
            dma((rounds, 2)),
            dma((rounds, 2)),
            dma((n - 1,)),
            dma((n - 1,)),
            dma,
            dma,
        ],
        compiler_params=pltpu.CompilerParams(
            collective_id=0, has_side_effects=True, vmem_limit_bytes=62 * 1024 * 1024
        ),
    )(
        screened,
        elements,
        node_freq[None, :],
        node_weight[None, :],
        band_energy[None, :],
        energy_grid[None, :],
        pair_state[None, :],
        pair_band[None, :],
    )


def per_device(
    screened, elements, node_freq, node_weight, band_energy, energy_grid, pair_state, pair_band
):
    n = lax.axis_size("row")
    two = n >= 4 and n % 2 == 0 and lax.axis_size("freq") == 2
    if two and elements.shape[2] % (2 * LANES) == 0 and elements.shape[1] % (2 * ROWS) == 0:
        return ring_sigma(
            screened, elements, node_freq, node_weight, band_energy, energy_grid, pair_state,
            pair_band,
        )
    w_real = screened[:, 0]
    w_imag = screened[:, 1]
    npair = elements.shape[1]
    half = npair // lax.axis_size("freq")
    mine = lax.dynamic_slice_in_dim(elements, lax.axis_index("freq") * half, half, 1)
    collected = lax.all_gather(mine, "row", axis=2, tiled=True)
    piece = lax.all_gather(collected, "freq", axis=1, tiled=True)
    part_real = product(w_real, piece[0]) - product(w_imag, piece[1])
    part_imag = product(w_real, piece[1]) + product(w_imag, piece[0])
    stacked = jnp.stack([part_real, part_imag])
    y_real = stacked[0]
    y_imag = stacked[1]
    own_real = elements[0].T.astype(jnp.float32)[None]
    own_imag = elements[1].T.astype(jnp.float32)[None]
    form_re = jnp.sum(own_real * y_real + own_imag * y_imag, axis=1)
    form_im = jnp.sum(own_real * y_imag - own_imag * y_real, axis=1)
    form_re, form_im = lax.psum((form_re, form_im), "row")
    partial_sigma = self_energy(
        form_re, form_im, node_freq, node_weight, band_energy, energy_grid, pair_state, pair_band
    )
    return lax.psum(partial_sigma, "freq")


def solution(mesh):
    in_specs = (
        P(("kpt", "freq"), None, "row", None),
        P(None, "kpt", "row"),
        P("freq"),
        P("freq"),
        P("kpt"),
        P(),
        P("kpt"),
        P("kpt"),
    )
    out_specs = P(None, "kpt", None)
    return jax.shard_map(
        per_device, mesh=mesh, in_specs=in_specs, out_specs=out_specs, check_vma=False
    )
```

time: 125 us -> 107 us (0.86)
  Pallas kernels: 118 us -> 106 us
  other arithmetic: 2.52 us -> 0 us
  matrix products: 1.7 us -> 0 us
    pallas_call x1, Pallas kernels: 118 us -> 106 us  [ring_sigma(): pl.pallas_call(functools.partial(forms_kernel, n, nodes, npair, block, LA...]
    dot_general x3 -> x0, matrix products: 1.7 us -> none  [the longest x1 1.31 us: self_energy(): jnp.dot(band_onehot, band_energy, precision=lax.Precision.HIGHEST)]
where the time goes in v1:
time: 107 us
  Pallas kernels  106 us (99%)
  local copies, waits for them, and re-layouts  1.38 us (1%)
    pallas_call x1, Pallas kernels, ring_sigma(): pl.pallas_call(functools.partial(forms_kernel, n, nodes, npair, block, LA...  106 us

profile of v1, /device:TPU:0, one launch (start us, length us, event | category | flops | bytes accessed | tf_op | source)
XLA Modules:
  0.0 107.0 jit_solution(3930251576852017189)
XLA Ops:
  0.0 105.6 %shard_map.82 = f32[2,32,64]{2,1,0:T(8,128)} custom-call(bf16[2,2,1024,8192]{3,2,1,0:T(8,128)(2,1)} %w_hbm.1, bf16[2,512,1024]{2,1,0:T(8,128)(2,1)} %m_hbm.1, f32[1,2]{1,0:T(1,128)} %bitcast.9, f32[1,2]{1,0:T(1,128)} %bitcast.10, f32[1,512]{1,0:T(1,128)} %bitcast.6, f32[1,64]{1,0:T(1,128)} %bitcast.11, s32[1,512]{1,0:T(1,128)} %bitcast.7, s32[1,512]{1,0:T(1,128)} %bitcast.8), custom_call_target="tpu_custom_call" | custom-call | tf_op jit(solution)/shard_map/pallas_call | solution.py:371
  105.6 1.4 %copy.10 = f32[2,32,64]{2,1,0:T(8,128)} copy(f32[2,32,64]{2,1,0:T(8,128)} %shard_map.82) | data formatting | bytes 32768

commit v2 on v1

--- a/solution.py
+++ b/solution.py
@@ -9,7 +9,7 @@
 
 NSTATE = 32
 LANES = 256
-ROWS = 64
+ROWS = 32
 MESH = pl.DeviceIdType.MESH
 NT = (((1,), (1,)), ((), ()))
 
@@ -63,9 +63,9 @@
     n, nodes, npair, block, lanes, lines,
     w_hbm, m_hbm, freq_hbm, weight_hbm, band_hbm, grid_hbm, state_hbm, pband_hbm,
     out_ref,
-    lhs, held, wbuf, zbuf, acc, factor, onehot, forms, peers, twin,
+    neg, held, wbuf, zbuf, acc, factor, onehot, forms, peers, twin,
     freq_v, weight_v, band_v, grid_v, state_v, pband_v,
-    small_sem, lhs_sem, own_sem, other_sem, w_sem,
+    small_sem, own_sem, other_sem, w_sem,
     send_sem, recv_sem, sib_send, sib_recv, form_send, form_recv, twin_send, twin_recv,
 ):
     me = lax.axis_index("row")
@@ -145,16 +145,8 @@
     order = [p * subs + k for k in range(subs) for p in range(2)]
     for q in order:
         own_copy(q, core, own_sem).start()
-    lhs_copies = [
-        pltpu.make_async_copy(
-            m_hbm.at[c], lhs.at[0, :, pl.ds(c * block, block)], lhs_sem.at[c]
-        )
-        for c in range(2)
-    ]
-    for copy in lhs_copies:
-        copy.start()
-    for copy in w_copies(0):
-        copy.start()
+    for q in order:
+        own_copy(q, other, other_sem).start()
     smalls = [
         pltpu.make_async_copy(src, dst, small_sem.at[i])
         for i, (src, dst) in enumerate(
@@ -166,18 +158,13 @@
     ]
     for copy in smalls:
         copy.start()
-    for q in order:
-        own_copy(q, other, other_sem).start()
+    for copy in w_copies(0):
+        copy.start()
     pl.semaphore_wait(barrier, 3)
 
     for q in order:
         own_copy(q, core, own_sem).wait()
-        for step in (1, 2):
-            for way in (0, 1):
-                first = (step + 1) % 2
-                part = first if way == 0 else 1 - first
-                if q // subs == part:
-                    send(step * subs + q % subs, way, me, q).start()
+        send(subs + q % subs, q // subs, me, q).start()
 
     for copy in smalls:
         copy.wait()
@@ -203,12 +190,11 @@
     onehot[...] = jnp.where(state_of == state_v[...], 1.0, 0.0).astype(jnp.bfloat16)
     acc[...] = jnp.zeros_like(acc)
 
-    for copy in lhs_copies:
-        copy.wait()
-    lhs[1, :, :block] = -lhs[0, :, block:]
-    lhs[1, :, block:] = lhs[0, :, :block]
     for q in order:
         own_copy(q, other, other_sem).wait()
+    for q in range(2 * subs):
+        for f in range(2):
+            neg[q, f] = -held[me, q, f, 1]
 
     def transfers(rnd):
         got = rnd - 1
@@ -218,12 +204,13 @@
             for way in (0, 1):
                 owner, q = piece_of(got, way)
                 send(got, way, owner, q).wait_recv()
-
-                @pl.when(got + 2 * subs < rounds)
-                def _():
-                    send(got + 2 * subs, way, owner, q).start()
-
                 pass_over(got, way, owner, q, core).start()
+
+        @pl.when((got >= 0) & (got + 2 * subs < rounds))
+        def _():
+            for way in (0, 1):
+                owner, q = piece_of(got, way)
+                send(got + 2 * subs, way, owner, q).start()
 
         done = rnd - 2
 
@@ -233,83 +220,90 @@
                 owner, q = piece_of(done, way)
                 pass_over(done, way, owner, q, other).wait_recv()
 
-    def weights(rnd):
+    def prefetch(rnd):
         @pl.when(rnd + 1 < rounds)
         def _():
             for copy in w_copies(rnd + 1):
                 copy.start()
 
+    def multiply(rnd, way, v, f):
+        total = 0.0
+        for c in range(2):
+            for q in range(2 * subs):
+                left_side = neg[q, f] if (v, c) == (1, 0) else held[me, q, f, c * (1 - v)]
+                right_side = wbuf[rnd % 2, way, pl.ds(c * block + q * lanes, lanes)]
+                total += jnp.dot(left_side, right_side, preferred_element_type=jnp.float32)
+        zbuf[rnd % 3, way, v, pl.ds(f * half, half)] = total
+
+    def combine(rnd, f, t):
+        slot = rnd % 3
+        spots = pl.ds(t * ROWS, ROWS)
+        pairs = pl.ds(f * half + t * ROWS, ROWS)
+        sums = [[0.0] * nodes for _ in range(2)]
+        for way in (0, 1):
+            owner, q = piece_of(rnd, way)
+            for i in range(lanes // 128):
+                cut = slice(i * 128, (i + 1) * 128)
+                r = held[owner, q, f, 0, spots, cut].astype(jnp.float32)
+                s = held[owner, q, f, 1, spots, cut].astype(jnp.float32)
+                for j in range(nodes):
+                    cut = slice(j * lanes + i * 128, j * lanes + (i + 1) * 128)
+                    zr = zbuf[slot, way, 0, pairs, cut]
+                    zi = zbuf[slot, way, 1, pairs, cut]
+                    sums[0][j] += zr * r - zi * s
+                    sums[1][j] += zr * s + zi * r
+        for j in range(nodes):
+            acc[0, j, pairs, :] += sums[0][j]
+            acc[1, j, pairs, :] += sums[1][j]
+
+    tiles = [
+        (way, v, f) for way in (0, 1) for f in range(2) for v in range(2)
+    ]
+    strips = [(f, t) for f in range(2) for t in range(half // ROWS)]
+
+    def opening(rnd, carry):
+        transfers(rnd)
+        prefetch(rnd)
+        copies = w_copies(rnd)
+        each = len(copies) // 2
+        for way in (0, 1):
+            for copy in copies[way * each : (way + 1) * each]:
+                copy.wait()
+            for tile in tiles:
+                if tile[0] == way:
+                    multiply(rnd, *tile)
+        return carry
+
+    def middle(rnd, carry):
+        transfers(rnd)
+        prefetch(rnd)
         for copy in w_copies(rnd):
             copy.wait()
-
-    def multiply(rnd):
-        for way in (0, 1):
-            for v in range(2):
-                zbuf[rnd % 2, way, v] = jnp.dot(
-                    lhs[v], wbuf[rnd % 2, way], preferred_element_type=jnp.float32
-                )
-
-    def combine(rnd):
-        for way in (0, 1):
-            owner, q = piece_of(rnd, way)
-            for f in range(2):
-                for t in range(half // ROWS):
-                    spots = pl.ds(t * ROWS, ROWS)
-                    pairs = pl.ds(f * half + t * ROWS, ROWS)
-                    r = held[owner, q, f, 0, spots, :].astype(jnp.float32)
-                    s = held[owner, q, f, 1, spots, :].astype(jnp.float32)
-                    for j in range(nodes):
-                        zr = zbuf[rnd % 2, way, 0, pairs, j * lanes : (j + 1) * lanes]
-                        zi = zbuf[rnd % 2, way, 1, pairs, j * lanes : (j + 1) * lanes]
-                        re = zr * r - zi * s
-                        im = zr * s + zi * r
-                        acc[0, j, pairs, :] += sum(
-                            re[:, i * 128 : (i + 1) * 128] for i in range(lanes // 128)
-                        )
-                        acc[1, j, pairs, :] += sum(
-                            im[:, i * 128 : (i + 1) * 128] for i in range(lanes // 128)
-                        )
-
-    def opening(rnd, carry):
-        transfers(rnd)
-        weights(rnd)
-        multiply(rnd)
-        return carry
-
-    def middle(rnd, carry):
-        transfers(rnd)
-        weights(rnd)
-        combine(rnd - 2)
-        multiply(rnd)
+        for i, tile in enumerate(tiles):
+            multiply(rnd, *tile)
+            for strip in strips[i * len(strips) // len(tiles) : (i + 1) * len(strips) // len(tiles)]:
+                combine(rnd - 2, *strip)
         return carry
 
     def closing(rnd, carry):
         transfers(rnd)
-        combine(rnd - 2)
+        for strip in strips:
+            combine(rnd - 2, *strip)
         return carry
 
     lax.fori_loop(0, 2, opening, 0)
     lax.fori_loop(2, rounds, middle, 0)
     lax.fori_loop(rounds, rounds + 2, closing, 0)
 
-    line_of = lax.broadcasted_iota(jnp.int32, (lines, 3 * 128), 0)
+    line_of = lax.broadcasted_iota(jnp.int32, (lines, 2 * 128), 0)
     total = jnp.zeros((lines, half), jnp.float32)
     for c in range(2):
         for j in range(nodes):
             for f in range(2):
-                parts = jnp.concatenate(thirds(acc[c, j, f * half : (f + 1) * half, :]), axis=1)
+                parts = jnp.concatenate(thirds(acc[c, j, f * half : (f + 1) * half, :])[:2], axis=1)
                 pick = jnp.where(line_of == (c * nodes + j) * 2 + f, 1.0, 0.0).astype(jnp.bfloat16)
                 total += lax.dot_general(pick, parts, NT, preferred_element_type=jnp.float32)
     forms[...] = total
-
-    def drain(rnd, carry):
-        for way in (0, 1):
-            owner, q = piece_of(rnd, way)
-            send(rnd, way, owner, q).wait_send()
-            pass_over(rnd, way, owner, q, core).wait_send()
-        return carry
-
-    lax.fori_loop(subs, rounds, drain, 0)
 
     def spread(hop):
         return pltpu.make_async_remote_copy(
@@ -323,6 +317,15 @@
 
     for hop in range(1, n):
         spread(hop).start()
+
+    def drain(rnd, carry):
+        for way in (0, 1):
+            owner, q = piece_of(rnd, way)
+            send(rnd, way, owner, q).wait_send()
+            pass_over(rnd, way, owner, q, core).wait_send()
+        return carry
+
+    lax.fori_loop(subs, rounds, drain, 0)
     total = forms[...]
     for hop in range(1, n):
         spread(hop).wait()
@@ -374,10 +377,10 @@
         in_specs=[pl.BlockSpec(memory_space=pl.ANY)] * 8,
         out_specs=pl.BlockSpec(memory_space=pltpu.VMEM),
         scratch_shapes=[
-            pltpu.VMEM((2, npair, 2 * block), jnp.bfloat16),
+            pltpu.VMEM((pieces, 2, half, LANES), jnp.bfloat16),
             pltpu.VMEM((n, pieces, 2, 2, half, LANES), jnp.bfloat16),
             pltpu.VMEM((2, 2, 2 * block, nodes * LANES), jnp.bfloat16),
-            pltpu.VMEM((2, 2, 2, npair, nodes * LANES), jnp.float32),
+            pltpu.VMEM((3, 2, 2, npair, nodes * LANES), jnp.float32),
             pltpu.VMEM((2, nodes, npair, 128), jnp.float32),
             pltpu.VMEM((nodes, ne, npair), jnp.float32),
             pltpu.VMEM((NSTATE, npair), jnp.bfloat16),
@@ -391,7 +394,6 @@
             pltpu.VMEM((1, npair), jnp.int32),
             pltpu.VMEM((1, npair), jnp.int32),
             dma((6,)),
-            dma((2,)),
             dma((pieces,)),
             dma((pieces,)),
             dma((2, 2, nodes, 2)),

time: 107 us -> 99.1 us (0.926)
  Pallas kernels: 106 us -> 97.5 us
    pallas_call x1, Pallas kernels: 106 us -> 97.5 us  [ring_sigma(): pl.pallas_call(functools.partial(forms_kernel, n, nodes, npair, block, LA...]
where the time goes in v2:
time: 99.1 us; the launch traced here: 98.9 us
  Pallas kernels  97.5 us (98%)
  local copies, waits for them, and re-layouts  1.38 us (1%)
    pallas_call x1, Pallas kernels, ring_sigma(): pl.pallas_call(functools.partial(forms_kernel, n, nodes, npair, block, LA...  97.5 us

profile of v2, /device:TPU:0, one launch (start us, length us, event | category | flops | bytes accessed | tf_op | source)
XLA Modules:
  0.0 98.9 jit_solution(134069102187260030)
XLA Ops:
  0.0 97.5 %shard_map.82 = f32[2,32,64]{2,1,0:T(8,128)} custom-call(bf16[2,2,1024,8192]{3,2,1,0:T(8,128)(2,1)} %w_hbm.1, bf16[2,512,1024]{2,1,0:T(8,128)(2,1)} %m_hbm.1, f32[1,2]{1,0:T(1,128)} %bitcast.9, f32[1,2]{1,0:T(1,128)} %bitcast.10, f32[1,512]{1,0:T(1,128)} %bitcast.6, f32[1,64]{1,0:T(1,128)} %bitcast.11, s32[1,512]{1,0:T(1,128)} %bitcast.7, s32[1,512]{1,0:T(1,128)} %bitcast.8), custom_call_target="tpu_custom_call" | custom-call | tf_op jit(solution)/shard_map/pallas_call | solution.py:374
  97.5 1.4 %copy.10 = f32[2,32,64]{2,1,0:T(8,128)} copy(f32[2,32,64]{2,1,0:T(8,128)} %shard_map.82) | data formatting | bytes 32768
